TPU v7x, 32 devices: a whole 2x2x4 slice. The times are simulated.
32 devices in a mesh: row: 8 (over z, x), col: 4 (over y, core).
Axes of the slice: x: 2, y: 2, z: 4, core: 2. Of those that a mesh axis runs over, the one named last changes fastest.
Arguments:
- state: bfloat16 [256, 16384], P(None, ('row', 'col')), may hold values from -0.94921875 to 0.94921875
- adjoint: bfloat16 [256, 16384], P(None, ('col', 'row')), may hold values from -6 to 6
- features: bfloat16 [128, 16384], P(None, ('col', 'row')), may hold values from -6 to 6
- cotangent: bfloat16 [256, 16384], P(None, ('row', 'col')), may hold values from -6 to 6
- mixing: bfloat16 [256, 256], replicated, may hold values from -0.375 to 0.375
- input_weight: bfloat16 [256, 128], replicated, may hold values from -0.5 to 0.5
- tiles: bfloat16 [8, 4, 170, 128, 128], P('row', 'col'), may hold values from -0.09375 to 0.09375
- tile_rows: int32 [8, 4, 170], P('row', 'col'), may hold values from 0 to 15, as said below
- tile_cols: int32 [8, 4, 170], P('row', 'col'), may hold values from 0 to 31, as said below
- live_tiles: int32 [8, 4], P('row', 'col'), may hold values from 85 to 170, as said below
Outputs:
- new_state: bfloat16 [256, 16384], P(None, ('col', 'row'))
- new_adjoint: bfloat16 [256, 16384], P(None, ('row', 'col'))
Inputs may be any that keep to these rules, and one draw needn't show every extreme that they name: On one device the pairs (tile_rows, tile_cols) of its 170 slots are all different. `tile_cols`: see tile_rows. `live_tiles`: some device has all 170 slots live.
All inputs are finite; a program needn't handle non-finite values.
Results may differ from a plain program's by a relative error of at most 0.014.
Values may be sent and summed in bfloat16 or wider, within the bound.
No kernel may reach another device: no remote copies, remote signals or barrier semaphores. Data moves between devices by JAX's collectives and lax.ppermute only.
A program may use at most 64 MiB of HBM per device.

v0:
```python
import functools

import jax
import jax.numpy as jnp
from jax import lax
from jax.experimental import pallas as pl
from jax.experimental.pallas import tpu as pltpu
from jax.sharding import PartitionSpec as P


VMEM = pltpu.VMEM
BF16 = jnp.bfloat16
F32 = jnp.float32
NT = (((1,), (1,)), ((), ()))
TN = (((0,), (0,)), ((), ()))


def in_vmem():
    return pl.BlockSpec(memory_space=VMEM)


def swap(value, axis, size, mask):
    return lax.ppermute(value, axis, [(i, i ^ mask) for i in range(size)])


def build_kernel(groups, here, rows, cols, count, tiles, dense, held, sems):
    slots, side, _ = held.shape
    group = slots // groups
    height, width = dense.shape

    def fetch(g):
        part = pl.ds(g * group, group)
        return pltpu.make_async_copy(tiles.at[part], held.at[part], sems.at[g])

    for g in range(groups):
        fetch(g).start()

    def clear(i, carry):
        dense[pl.ds(pl.multiple_of(i * 32, 32), 32), :] = jnp.zeros((32, width), dense.dtype)
        return carry

    lax.fori_loop(0, height // 32, clear, 0)

    def place(slot, carry):
        r, c = rows[slot], cols[slot]
        r = pl.multiple_of((r ^ here[1]) * side, side)
        c = pl.multiple_of((c ^ here[0]) * side, side)
        dense[pl.ds(r, side), pl.ds(c, side)] = held[slot]
        return carry

    for g in range(groups):
        fetch(g).wait()
        lax.fori_loop(g * group, jnp.clip(count[0], g * group, (g + 1) * group), place, 0)


def build(here, rows, cols, count, tiles, height, width):
    slots = tiles.shape[0]
    groups = max(g for g in range(1, 11) if slots % g == 0)
    smem = pl.BlockSpec(memory_space=pltpu.SMEM)
    return pl.pallas_call(
        functools.partial(build_kernel, groups),
        in_specs=[smem] * 4 + [pl.BlockSpec(memory_space=pltpu.HBM)],
        out_specs=in_vmem(),
        out_shape=jax.ShapeDtypeStruct((height, width), BF16),
        scratch_shapes=[VMEM(tiles.shape, BF16), pltpu.SemaphoreType.DMA((groups,))],
        compiler_params=pltpu.CompilerParams(vmem_limit_bytes=8 * 2**20),
        cost_estimate=pl.CostEstimate(flops=5 * 10**9, bytes_accessed=tiles.size * 2, transcendentals=0),
        name="build",
    )(here, rows, cols, count, tiles)


def forward_kernel(parts, extra, *refs):
    blocks, dense, rest = refs[:parts], refs[parts], refs[parts + 1 :]
    picks, rest = rest[:extra], rest[extra:]
    outs, whole = rest[:-1], rest[-1]
    width = blocks[0].shape[1]
    for k in range(parts):
        whole[:, k * width : (k + 1) * width] = blocks[k][...]
    first = 1
    if extra:
        weight, features = picks
        outs[-1][...] = jnp.dot(weight[...], features[...], preferred_element_type=F32)
        outs, first = outs[:-1], 0
    span = outs[0].shape[1]
    for j, out in enumerate(outs):
        start = (2 * j + first) * span
        out[...] = jnp.dot(
            whole[...], dense[:, start : start + span], preferred_element_type=F32
        ).astype(BF16)


def backward_kernel(parts, extra, *refs):
    blocks, dense, rest = refs[:parts], refs[parts], refs[parts + 1 :]
    picks, rest = rest[:extra], rest[extra:]
    outs, whole = rest[:-1], rest[-1]
    width = blocks[0].shape[1]
    for k in range(parts):
        whole[:, k * width : (k + 1) * width] = blocks[k][...]
    first = 0 if extra else 1
    span = outs[0].shape[1]
    for j, out in enumerate(outs):
        start = (2 * j + first) * span
        total = lax.dot_general(
            whole[...], dense[start : start + span, :], NT, preferred_element_type=F32
        )
        if extra and j:
            total = total + picks[j - 1][...].astype(F32)
        out[...] = total.astype(BF16)


def multiply(kernel, blocks, dense, picks, outs):
    hidden, width = blocks[0].shape
    parts = len(blocks)
    return pl.pallas_call(
        functools.partial(kernel, parts, len(picks)),
        in_specs=[in_vmem()] * (parts + 1 + len(picks)),
        out_specs=[in_vmem()] * len(outs),
        out_shape=outs,
        scratch_shapes=[VMEM((hidden, parts * width), BF16)],
        compiler_params=pltpu.CompilerParams(vmem_limit_bytes=8 * 2**20),
        cost_estimate=pl.CostEstimate(flops=hidden * dense.size, bytes_accessed=dense.size, transcendentals=0),
    )(*blocks, dense, *picks)


def state_kernel(terms, *refs):
    flow = refs[0][...].astype(F32)
    for ref in refs[1:terms]:
        flow = flow + ref[...].astype(F32)
    mixing, base, out = refs[terms:]
    pre = base[...] + jnp.dot(mixing[...], flow.astype(BF16), preferred_element_type=F32)
    out[...] = jnp.tanh(pre).astype(BF16)


def adjoint_kernel(terms, *refs):
    back = refs[0][...].astype(F32)
    for ref in refs[1:terms]:
        back = back + ref[...].astype(F32)
    mixing, state, cotangent, out = refs[terms:]
    pulled = lax.dot_general(mixing[...], back.astype(BF16), TN, preferred_element_type=F32)
    wide = state[...].astype(F32)
    out[...] = ((1.0 - wide * wide) * (pulled + cotangent[...].astype(F32))).astype(BF16)


def finish(kernel, terms, others):
    return pl.pallas_call(
        functools.partial(kernel, len(terms)),
        in_specs=[in_vmem()] * (len(terms) + len(others)),
        out_specs=in_vmem(),
        out_shape=jax.ShapeDtypeStruct(terms[0].shape, BF16),
        compiler_params=pltpu.CompilerParams(vmem_limit_bytes=4 * 2**20),
        cost_estimate=pl.CostEstimate(flops=10**9, bytes_accessed=2**21, transcendentals=0),
    )(*terms, *others)


def per_device(state, adjoint, features, cotangent, mixing, input_weight, tiles, tile_rows, tile_cols, live_tiles):
    n_row, n_col = lax.axis_size("row"), lax.axis_size("col")
    my_row, my_col = lax.axis_index("row"), lax.axis_index("col")
    hidden, nodes = state.shape
    slab = tiles[0, 0]
    side = slab.shape[-1]
    per_chunk = nodes // side
    here = jnp.stack([my_row * per_chunk, my_col * per_chunk]).astype(jnp.int32)
    half_row, half_col = n_row // 2, n_col // 2
    piece = jax.ShapeDtypeStruct((hidden, nodes), BF16)
    wide = jax.ShapeDtypeStruct((hidden, nodes), F32)

    def by_row(value, mask):
        return swap(value, "row", n_row, mask)

    def by_col(value, mask):
        return swap(value, "col", n_col, mask)

    near = [adjoint]
    for k in range(1, half_row):
        far = k > 1 and k % 2
        near.append(by_row(near[k - 1] if far else adjoint, 2 if far else 2 * k))
    adjoints = []
    for block in near:
        adjoints += [block, by_row(block, 1)]

    near = [state] + [by_col(state, 2 * k) for k in range(1, half_col)]
    states = []
    for block in near:
        states += [block, by_col(block, 1)]

    dense = build(here, tile_rows[0, 0], tile_cols[0, 0], live_tiles[0], slab, n_col * nodes, n_row * nodes)

    others = multiply(forward_kernel, states, dense, (), [piece] * half_row)
    others = [by_row(others[k], 1) for k in range(half_row)]
    mine = multiply(forward_kernel, states, dense, (input_weight, features), [piece] * half_row + [wide])
    *mine, base = mine
    flows = [mine[0], others[0]]
    relayed = None
    for k in reversed(range(1, half_row)):
        pair = mine[k].astype(F32) + others[k].astype(F32)
        if relayed is not None:
            pair = pair + relayed.astype(F32)
        far = k > 1 and k % 2
        moved = by_row(pair.astype(BF16), 2 if far else 2 * k)
        relayed = moved if far else None
        if not far:
            flows.append(moved)
    new_state = finish(state_kernel, flows, (mixing, base))

    others = multiply(backward_kernel, adjoints, dense, (), [piece] * half_col)
    others = [by_col(others[k], 1) for k in range(half_col)]
    mine = multiply(backward_kernel, adjoints, dense, others[1:], [piece] * half_col)
    backs = [mine[0], others[0]] + [by_col(mine[k], 2 * k) for k in range(1, half_col)]
    new_adjoint = finish(adjoint_kernel, backs, (mixing, state, cotangent))
    return (new_state, new_adjoint)


def solution(mesh):
    placed = (
        P(None, ("row", "col")),
        P(None, ("col", "row")),
        P(None, ("col", "row")),
        P(None, ("row", "col")),
        P(),
        P(),
        P("row", "col", None, None, None),
        P("row", "col", None),
        P("row", "col", None),
        P("row", "col"),
    )
    return jax.shard_map(
        per_device,
        mesh=mesh,
        in_specs=placed,
        out_specs=(P(None, ("col", "row")), P(None, ("row", "col"))),
        check_vma=False,
    )
```

profile of v0, /device:TPU:0, one launch (start us, length us, event | category | flops | bytes accessed | tf_op | source)
XLA Modules:
  0.0 89.3 jit_solution(1403131489073389347)
XLA Ops:
  0.6 3.1 %collective-permute-start.1 = (bf16[256,512]{1,0:T(8,128)(2,1)}, bf16[256,512]{1,0:T(8,128)(2,1)S(1)}, u32[]{:S(2)}, u32[]{:S(2)}) collective-permute-start(bf16[256,512]{1,0:T(8,128)(2,1)} %refs_4_.3), channel_id=1, source_target_pairs={{0,2},{1,3},{2,0},{3,1},{4,6},{5,7},{6,4},{7,5},{8,10},{9,11},{10,... | collective-permute-start | bytes 786440 | tf_op jit(solution)/shard_map/ppermute | solution.py:23
  3.7 2.6 %collective-permute-start.13 = (bf16[256,512]{1,0:T(8,128)(2,1)}, bf16[256,512]{1,0:T(8,128)(2,1)S(1)}, u32[]{:S(2)}, u32[]{:S(2)}) collective-permute-start(bf16[256,512]{1,0:T(8,128)(2,1)} %refs_0_.7), channel_id=1, source_target_pairs={{0,16},{4,20},{8,24},{12,28},{16,0},{20,4},{24,8},{28,12},{1,17},{... | collective-permute-start | bytes 786440 | tf_op jit(solution)/shard_map/ppermute | solution.py:23
  6.3 1.5 %collective-permute-start.10 = (bf16[256,512]{1,0:T(8,128)(2,1)}, bf16[256,512]{1,0:T(8,128)(2,1)S(1)}, u32[]{:S(2)}, u32[]{:S(2)}) collective-permute-start(bf16[256,512]{1,0:T(8,128)(2,1)} %refs_0_.7), channel_id=1, source_target_pairs={{0,4},{4,0},{8,12},{12,8},{16,20},{20,16},{24,28},{28,24},{1,5},{5... | collective-permute-start | bytes 786440 | tf_op jit(solution)/shard_map/ppermute | solution.py:23
  7.8 1.6 %collective-permute-start.11 = (bf16[256,512]{1,0:T(8,128)(2,1)}, bf16[256,512]{1,0:T(8,128)(2,1)S(1)}, u32[]{:S(2)}, u32[]{:S(2)}) collective-permute-start(bf16[256,512]{1,0:T(8,128)(2,1)} %refs_0_.7), channel_id=1, source_target_pairs={{0,8},{4,12},{8,0},{12,4},{16,24},{20,28},{24,16},{28,20},{1,9},{5... | collective-permute-start | bytes 786440 | tf_op jit(solution)/shard_map/ppermute | solution.py:23
  10.2 8.1 %collective-permute-done.13.refs_4_ = bf16[256,512]{1,0:T(8,128)(2,1)S(1)} collective-permute-done((bf16[256,512]{1,0:T(8,128)(2,1)}, bf16[256,512]{1,0:T(8,128)(2,1)S(1)}, u32[]{:S(2)}, u32[]{:S(2)}) %collective-permute-start.13) | collective-permute-done | bytes 262176 | tf_op jit(solution)/shard_map/ppermute | solution.py:23
  18.3 0.7 collective-permute-start.15
  19.0 2.6 %copy-done = bf16[1,1,170,128,128]{4,3,2,1,0:T(8,128)(2,1)S(1)} copy-done((bf16[1,1,170,128,128]{4,3,2,1,0:T(8,128)(2,1)S(1)}, bf16[1,1,170,128,128]{4,3,2,1,0:T(8,128)(2,1)}, u32[]{:S(2)}) %copy-start) | copy-done | bytes 5570584
  21.6 0.7 copy-done.5
  22.3 0.7 copy-done.6
  23.0 4.2 %build.1.refs_4_.refs_8_ = bf16[2048,4096]{1,0:T(8,128)(2,1)S(1)} custom-call(s32[2]{0:T(128)S(1)} %pad_add_fusion.here, s32[170]{0:T(256)S(1)} %bitcast.8, s32[170]{0:T(256)S(1)} %bitcast.9, s32[1]{0:T(128)} %bitcast.6.count, bf16[170,128,128]{2,1,0:T(8,128)(2,1)S(1)} %bitcast.7), custom_call_target="tpu_custom_call" | custom-call | flops 5000000000 | bytes 5570560 | tf_op jit(solution)/shard_map/build/pallas_call | solution.py:60
  27.2 2.0 %collective-permute-start.14 = (bf16[256,512]{1,0:T(8,128)(2,1)S(1)}, bf16[256,512]{1,0:T(8,128)(2,1)S(1)}, u32[]{:S(2)}, u32[]{:S(2)}) collective-permute-start(bf16[256,512]{1,0:T(8,128)(2,1)S(1)} %collective-permute-done.13.refs_4_), channel_id=1, source_target_pairs={{0,4},{4,0},{8,12},{12,8},{16,20},{20,16},{24,28},{28,24},{1,5},{5... | collective-permute-start | bytes 786440 | tf_op jit(solution)/shard_map/ppermute | solution.py:23
  29.3 1.9 %collective-permute-start.16 = (bf16[256,512]{1,0:T(8,128)(2,1)S(1)}, bf16[256,512]{1,0:T(8,128)(2,1)S(1)}, u32[]{:S(2)}, u32[]{:S(2)}) collective-permute-start(bf16[256,512]{1,0:T(8,128)(2,1)S(1)} %collective-permute-done.15.refs_6_), channel_id=1, source_target_pairs={{0,4},{4,0},{8,12},{12,8},{16,20},{20,16},{24,28},{28,24},{1,5},{5... | collective-permute-start | bytes 786440 | tf_op jit(solution)/shard_map/ppermute | solution.py:23
  31.2 2.4 %shard_map.114 = (bf16[256,512]{1,0:T(8,128)(2,1)S(1)}, bf16[256,512]{1,0:T(8,128)(2,1)S(1)}, bf16[256,512]{1,0:T(8,128)(2,1)S(1)}, bf16[256,512]{1,0:T(8,128)(2,1)S(1)}) custom-call(bf16[256,512]{1,0:T(8,128)(2,1)S(1)} %copy-done.2, bf16[256,512]{1,0:T(8,128)(2,1)S(1)} %collective-permute-done.refs_1_, bf16[256,512]{1,0:T(8,128)(2,1)S(1)} %collective-permute-done.1.refs_2_, ...), custom_call_target="tpu_custom_call" | custom-call | flops 2147483648 | bytes 8388608 | tf_op jit(solution)/shard_map/pallas_call | solution.py:114
  33.6 0.2 collective-permute-start.5
  33.8 2.4 %shard_map.113 = (bf16[256,512]{1,0:T(8,128)(2,1)S(1)}, bf16[256,512]{1,0:T(8,128)(2,1)S(1)}, bf16[256,512]{1,0:T(8,128)(2,1)S(1)}, bf16[256,512]{1,0:T(8,128)(2,1)S(1)}, f32[256,512]{1,0:T(8,128)S(1)}) custom-call(bf16[256,512]{1,0:T(8,128)(2,1)S(1)} %copy-done.2, bf16[256,512]{1,0:T(8,128)(2,1)S(1)} %collective-permute-done.refs_1_, ...), custom_call_target="tpu_custom_call" | custom-call | flops 2147483648 | bytes 8388608 | tf_op jit(solution)/shard_map/pallas_call | solution.py:114
  36.2 2.0 %collective-permute-start.3 = (bf16[256,512]{1,0:T(8,128)(2,1)S(1)}, bf16[256,512]{1,0:T(8,128)(2,1)S(1)}, u32[]{:S(2)}, u32[]{:S(2)}) collective-permute-start(bf16[256,512]{1,0:T(8,128)(2,1)S(1)} %get-tuple-element.16), channel_id=1, source_target_pairs={{0,4},{4,0},{8,12},{12,8},{16,20},{20,16},{24,28},{28,24},{1,5},{5... | collective-permute-start | bytes 786440 | tf_op jit(solution)/shard_map/ppermute | solution.py:23
  38.2 3.9 %collective-permute-done.12.refs_3_ = bf16[256,512]{1,0:T(8,128)(2,1)S(1)} collective-permute-done((bf16[256,512]{1,0:T(8,128)(2,1)S(1)}, bf16[256,512]{1,0:T(8,128)(2,1)S(1)}, u32[]{:S(2)}, u32[]{:S(2)}) %collective-permute-start.12) | collective-permute-done | bytes 262176 | tf_op jit(solution)/shard_map/ppermute | solution.py:23
  42.0 1.9 %collective-permute-start.4 = (bf16[256,512]{1,0:T(8,128)(2,1)S(1)}, bf16[256,512]{1,0:T(8,128)(2,1)S(1)}, u32[]{:S(2)}, u32[]{:S(2)}) collective-permute-start(bf16[256,512]{1,0:T(8,128)(2,1)S(1)} %get-tuple-element.18), channel_id=1, source_target_pairs={{0,4},{4,0},{8,12},{12,8},{16,20},{20,16},{24,28},{28,24},{1,5},{5... | collective-permute-start | bytes 786440 | tf_op jit(solution)/shard_map/ppermute | solution.py:23
  43.9 0.2 collective-permute-start.8
  44.1 3.6 %collective-permute-done.16.refs_7_ = bf16[256,512]{1,0:T(8,128)(2,1)S(1)} collective-permute-done((bf16[256,512]{1,0:T(8,128)(2,1)S(1)}, bf16[256,512]{1,0:T(8,128)(2,1)S(1)}, u32[]{:S(2)}, u32[]{:S(2)}) %collective-permute-start.16) | collective-permute-done | bytes 262176 | tf_op jit(solution)/shard_map/ppermute | solution.py:23
  47.7 2.4 %shard_map.116 = (bf16[256,512]{1,0:T(8,128)(2,1)S(1)}, bf16[256,512]{1,0:T(8,128)(2,1)S(1)}) custom-call(bf16[256,512]{1,0:T(8,128)(2,1)S(1)} %copy-done.1, bf16[256,512]{1,0:T(8,128)(2,1)S(1)} %collective-permute-done.10.refs_1_, bf16[256,512]{1,0:T(8,128)(2,1)S(1)} %collective-permute-done.11.refs_2_, ...), custom_call_target="tpu_custom_call" | custom-call | flops 2147483648 | bytes 8388608 | tf_op jit(solution)/shard_map/pallas_call | solution.py:114
  50.1 3.2 %collective-permute-done.5 = bf16[256,512]{1,0:T(8,128)(2,1)S(1)} collective-permute-done((bf16[256,512]{1,0:T(8,128)(2,1)S(1)}, bf16[256,512]{1,0:T(8,128)(2,1)S(1)}, u32[]{:S(2)}, u32[]{:S(2)}) %collective-permute-start.5) | collective-permute-done | bytes 262176 | tf_op jit(solution)/shard_map/ppermute | solution.py:23
  53.3 1.1 %collective-permute-start.6 = (bf16[256,512]{1,0:T(8,128)(2,1)S(1)}, bf16[256,512]{1,0:T(8,128)(2,1)S(1)}, u32[]{:S(2)}, u32[]{:S(2)}) collective-permute-start(bf16[256,512]{1,0:T(8,128)(2,1)S(1)} %add_convert_fusion.2), channel_id=1, source_target_pairs={{0,8},{4,12},{8,0},{12,4},{16,24},{20,28},{24,16},{28,20},{1,9},{5... | collective-permute-start | bytes 786440 | tf_op jit(solution)/shard_map/ppermute | solution.py:23
  54.5 14.8 %collective-permute-done.8 = bf16[256,512]{1,0:T(8,128)(2,1)S(1)} collective-permute-done((bf16[256,512]{1,0:T(8,128)(2,1)S(1)}, bf16[256,512]{1,0:T(8,128)(2,1)S(1)}, u32[]{:S(2)}, u32[]{:S(2)}) %collective-permute-start.8) | collective-permute-done | bytes 262176 | tf_op jit(solution)/shard_map/ppermute | solution.py:23
  69.3 0.4 collective-permute-start.9
  69.7 2.4 %shard_map.117 = (bf16[256,512]{1,0:T(8,128)(2,1)S(1)}, bf16[256,512]{1,0:T(8,128)(2,1)S(1)}) custom-call(bf16[256,512]{1,0:T(8,128)(2,1)S(1)} %copy-done.1, bf16[256,512]{1,0:T(8,128)(2,1)S(1)} %collective-permute-done.10.refs_1_, bf16[256,512]{1,0:T(8,128)(2,1)S(1)} %collective-permute-done.11.refs_2_, ...), custom_call_target="tpu_custom_call" | custom-call | flops 2147483648 | bytes 8388608 | tf_op jit(solution)/shard_map/pallas_call | solution.py:114
  72.1 0.5 collective-permute-start.19
  72.7 2.9 %collective-permute-start.7 = (bf16[256,512]{1,0:T(8,128)(2,1)S(1)}, bf16[256,512]{1,0:T(8,128)(2,1)S(1)}, u32[]{:S(2)}, u32[]{:S(2)}) collective-permute-start(bf16[256,512]{1,0:T(8,128)(2,1)S(1)} %add_convert_fusion.1), channel_id=1, source_target_pairs={{0,16},{4,20},{8,24},{12,28},{16,0},{20,4},{24,8},{28,12},{1,17},{... | collective-permute-start | bytes 786440 | tf_op jit(solution)/shard_map/ppermute | solution.py:23
  75.7 5.2 %collective-permute-done.19.refs_2_ = bf16[256,512]{1,0:T(8,128)(2,1)S(1)} collective-permute-done((bf16[256,512]{1,0:T(8,128)(2,1)S(1)}, bf16[256,512]{1,0:T(8,128)(2,1)S(1)}, u32[]{:S(2)}, u32[]{:S(2)}) %collective-permute-start.19) | collective-permute-done | bytes 262176 | tf_op jit(solution)/shard_map/ppermute | solution.py:23
  80.9 1.0 %shard_map.118 = bf16[256,512]{1,0:T(8,128)(2,1)} custom-call(bf16[256,512]{1,0:T(8,128)(2,1)S(1)} %get-tuple-element.25.refs_0_, bf16[256,512]{1,0:T(8,128)(2,1)S(1)} %collective-permute-done.18.refs_1_, bf16[256,512]{1,0:T(8,128)(2,1)S(1)} %collective-permute-done.19.refs_2_, bf16[256,256]{1,0:T(8,128)(2,1)S(1)} %copy-done.8, ...), custom_call_target="tpu_custom_call" | custom-call | flops 1000000000 | bytes 2097152 | tf_op jit(solution)/shard_map/pallas_call | solution.py:145
  81.9 6.3 %collective-permute-done.7.refs_2_ = bf16[256,512]{1,0:T(8,128)(2,1)S(1)} collective-permute-done((bf16[256,512]{1,0:T(8,128)(2,1)S(1)}, bf16[256,512]{1,0:T(8,128)(2,1)S(1)}, u32[]{:S(2)}, u32[]{:S(2)}) %collective-permute-start.7) | collective-permute-done | bytes 262176 | tf_op jit(solution)/shard_map/ppermute | solution.py:23
  88.3 1.0 %shard_map.115 = bf16[256,512]{1,0:T(8,128)(2,1)} custom-call(bf16[256,512]{1,0:T(8,128)(2,1)S(1)} %get-tuple-element.15.refs_0_, bf16[256,512]{1,0:T(8,128)(2,1)S(1)} %collective-permute-done.3.refs_1_, bf16[256,512]{1,0:T(8,128)(2,1)S(1)} %collective-permute-done.7.refs_2_, bf16[256,512]{1,0:T(8,128)(2,1)S(1)} %collective-permute-done.9.refs_3_, ...), custom_call_target="tpu_custom_call" | custom-call | flops 1000000000 | bytes 2097152 | tf_op jit(solution)/shard_map/pallas_call | solution.py:145
  (37 shorter events, 0.7 us)
Async XLA Ops:
  0.6 9.6 %collective-permute-start.1 = (bf16[256,512]{1,0:T(8,128)(2,1)}, bf16[256,512]{1,0:T(8,128)(2,1)S(1)}, u32[]{:S(2)}, u32[]{:S(2)}) collective-permute-start(bf16[256,512]{1,0:T(8,128)(2,1)} %refs_4_.3), channel_id=1, source_target_pairs={{0,2},{1,3},{2,0},{3,1},{4,6},{5,7},{6,4},{7,5},{8,10},{9,11},{10,... | collective-permute-start | bytes 786440 | tf_op jit(solution)/shard_map/ppermute | solution.py:23
  3.7 14.6 %collective-permute-start.13 = (bf16[256,512]{1,0:T(8,128)(2,1)}, bf16[256,512]{1,0:T(8,128)(2,1)S(1)}, u32[]{:S(2)}, u32[]{:S(2)}) collective-permute-start(bf16[256,512]{1,0:T(8,128)(2,1)} %refs_0_.7), channel_id=1, source_target_pairs={{0,16},{4,20},{8,24},{12,28},{16,0},{20,4},{24,8},{28,12},{1,17},{... | collective-permute-start | bytes 786440 | tf_op jit(solution)/shard_map/ppermute | solution.py:23
  6.3 20.9 %collective-permute-start = (bf16[256,512]{1,0:T(8,128)(2,1)}, bf16[256,512]{1,0:T(8,128)(2,1)S(1)}, u32[]{:S(2)}, u32[]{:S(2)}) collective-permute-start(bf16[256,512]{1,0:T(8,128)(2,1)} %refs_4_.3), channel_id=1, source_target_pairs={{0,1},{1,0},{2,3},{3,2},{4,5},{5,4},{6,7},{7,6},{8,9},{9,8},{10,11... | collective-permute-start | bytes 786440 | tf_op jit(solution)/shard_map/ppermute | solution.py:23
  6.3 29.9 %collective-permute-start.10 = (bf16[256,512]{1,0:T(8,128)(2,1)}, bf16[256,512]{1,0:T(8,128)(2,1)S(1)}, u32[]{:S(2)}, u32[]{:S(2)}) collective-permute-start(bf16[256,512]{1,0:T(8,128)(2,1)} %refs_0_.7), channel_id=1, source_target_pairs={{0,4},{4,0},{8,12},{12,8},{16,20},{20,16},{24,28},{28,24},{1,5},{5... | collective-permute-start | bytes 786440 | tf_op jit(solution)/shard_map/ppermute | solution.py:23
  7.8 21.4 %collective-permute-start.11 = (bf16[256,512]{1,0:T(8,128)(2,1)}, bf16[256,512]{1,0:T(8,128)(2,1)S(1)}, u32[]{:S(2)}, u32[]{:S(2)}) collective-permute-start(bf16[256,512]{1,0:T(8,128)(2,1)} %refs_0_.7), channel_id=1, source_target_pairs={{0,8},{4,12},{8,0},{12,4},{16,24},{20,28},{24,16},{28,20},{1,9},{5... | collective-permute-start | bytes 786440 | tf_op jit(solution)/shard_map/ppermute | solution.py:23
  10.2 21.0 %collective-permute-start.2 = (bf16[256,512]{1,0:T(8,128)(2,1)S(1)}, bf16[256,512]{1,0:T(8,128)(2,1)S(1)}, u32[]{:S(2)}, u32[]{:S(2)}) collective-permute-start(bf16[256,512]{1,0:T(8,128)(2,1)S(1)} %collective-permute-done.1.refs_2_), channel_id=1, source_target_pairs={{0,1},{1,0},{2,3},{3,2},{4,5},{5,4},{6,7},{7,6},{8,9},{9,8},{10,11... | collective-permute-start | bytes 786440 | tf_op jit(solution)/shard_map/ppermute | solution.py:23
  18.3 11.0 %collective-permute-start.15 = (bf16[256,512]{1,0:T(8,128)(2,1)S(1)}, bf16[256,512]{1,0:T(8,128)(2,1)S(1)}, u32[]{:S(2)}, u32[]{:S(2)}) collective-permute-start(bf16[256,512]{1,0:T(8,128)(2,1)S(1)} %collective-permute-done.13.refs_4_), channel_id=1, source_target_pairs={{0,8},{4,12},{8,0},{12,4},{16,24},{20,28},{24,16},{28,20},{1,9},{5... | collective-permute-start | bytes 786440 | tf_op jit(solution)/shard_map/ppermute | solution.py:23
  19.0 2.6 %copy-start = (bf16[1,1,170,128,128]{4,3,2,1,0:T(8,128)(2,1)S(1)}, bf16[1,1,170,128,128]{4,3,2,1,0:T(8,128)(2,1)}, u32[]{:S(2)}) copy-start(bf16[1,1,170,128,128]{4,3,2,1,0:T(8,128)(2,1)} %param.16) | copy-start | bytes 16711684
  21.6 0.7 copy-start.5
  22.3 0.7 copy-start.6
  22.9 8.2 %copy-start.2 = (bf16[256,512]{1,0:T(8,128)(2,1)S(1)}, bf16[256,512]{1,0:T(8,128)(2,1)}, u32[]{:S(2)}) copy-start(bf16[256,512]{1,0:T(8,128)(2,1)} %refs_4_.3) | copy-start | bytes 786436
  22.9 10.8 %copy-start.3 = (bf16[128,512]{1,0:T(8,128)(2,1)S(1)}, bf16[128,512]{1,0:T(8,128)(2,1)}, u32[]{:S(2)}) copy-start(bf16[128,512]{1,0:T(8,128)(2,1)} %refs_6_.1) | copy-start | bytes 393220
  22.9 10.8 %copy-start.4 = (bf16[256,128]{1,0:T(8,128)(2,1)S(1)}, bf16[256,128]{1,0:T(8,128)(2,1)}, u32[]{:S(2)}) copy-start(bf16[256,128]{1,0:T(8,128)(2,1)} %refs_5_.2) | copy-start | bytes 196612
  27.2 20.5 %copy-start.1 = (bf16[256,512]{1,0:T(8,128)(2,1)S(1)}, bf16[256,512]{1,0:T(8,128)(2,1)}, u32[]{:S(2)}) copy-start(bf16[256,512]{1,0:T(8,128)(2,1)} %refs_0_.7) | copy-start | bytes 786436
  27.2 16.8 %collective-permute-start.14 = (bf16[256,512]{1,0:T(8,128)(2,1)S(1)}, bf16[256,512]{1,0:T(8,128)(2,1)S(1)}, u32[]{:S(2)}, u32[]{:S(2)}) collective-permute-start(bf16[256,512]{1,0:T(8,128)(2,1)S(1)} %collective-permute-done.13.refs_4_), channel_id=1, source_target_pairs={{0,4},{4,0},{8,12},{12,8},{16,20},{20,16},{24,28},{28,24},{1,5},{5... | collective-permute-start | bytes 786440 | tf_op jit(solution)/shard_map/ppermute | solution.py:23
  29.1 12.9 %collective-permute-start.12 = (bf16[256,512]{1,0:T(8,128)(2,1)S(1)}, bf16[256,512]{1,0:T(8,128)(2,1)S(1)}, u32[]{:S(2)}, u32[]{:S(2)}) collective-permute-start(bf16[256,512]{1,0:T(8,128)(2,1)S(1)} %collective-permute-done.11.refs_2_), channel_id=1, source_target_pairs={{0,4},{4,0},{8,12},{12,8},{16,20},{20,16},{24,28},{28,24},{1,5},{5... | collective-permute-start | bytes 786440 | tf_op jit(solution)/shard_map/ppermute | solution.py:23
  29.3 18.4 %collective-permute-start.16 = (bf16[256,512]{1,0:T(8,128)(2,1)S(1)}, bf16[256,512]{1,0:T(8,128)(2,1)S(1)}, u32[]{:S(2)}, u32[]{:S(2)}) collective-permute-start(bf16[256,512]{1,0:T(8,128)(2,1)S(1)} %collective-permute-done.15.refs_6_), channel_id=1, source_target_pairs={{0,4},{4,0},{8,12},{12,8},{16,20},{20,16},{24,28},{28,24},{1,5},{5... | collective-permute-start | bytes 786440 | tf_op jit(solution)/shard_map/ppermute | solution.py:23
  33.6 19.7 %collective-permute-start.5 = (bf16[256,512]{1,0:T(8,128)(2,1)S(1)}, bf16[256,512]{1,0:T(8,128)(2,1)S(1)}, u32[]{:S(2)}, u32[]{:S(2)}) collective-permute-start(bf16[256,512]{1,0:T(8,128)(2,1)S(1)} %get-tuple-element.20), channel_id=1, source_target_pairs={{0,4},{4,0},{8,12},{12,8},{16,20},{20,16},{24,28},{28,24},{1,5},{5... | collective-permute-start | bytes 786440 | tf_op jit(solution)/shard_map/ppermute | solution.py:23
  36.2 45.7 %collective-permute-start.3 = (bf16[256,512]{1,0:T(8,128)(2,1)S(1)}, bf16[256,512]{1,0:T(8,128)(2,1)S(1)}, u32[]{:S(2)}, u32[]{:S(2)}) collective-permute-start(bf16[256,512]{1,0:T(8,128)(2,1)S(1)} %get-tuple-element.16), channel_id=1, source_target_pairs={{0,4},{4,0},{8,12},{12,8},{16,20},{20,16},{24,28},{28,24},{1,5},{5... | collective-permute-start | bytes 786440 | tf_op jit(solution)/shard_map/ppermute | solution.py:23
  42.0 30.1 %collective-permute-start.4 = (bf16[256,512]{1,0:T(8,128)(2,1)S(1)}, bf16[256,512]{1,0:T(8,128)(2,1)S(1)}, u32[]{:S(2)}, u32[]{:S(2)}) collective-permute-start(bf16[256,512]{1,0:T(8,128)(2,1)S(1)} %get-tuple-element.18), channel_id=1, source_target_pairs={{0,4},{4,0},{8,12},{12,8},{16,20},{20,16},{24,28},{28,24},{1,5},{5... | collective-permute-start | bytes 786440 | tf_op jit(solution)/shard_map/ppermute | solution.py:23
  43.9 37.0 %copy-start.7 = (bf16[256,512]{1,0:T(8,128)(2,1)S(1)}, bf16[256,512]{1,0:T(8,128)(2,1)}, u32[]{:S(2)}) copy-start(bf16[256,512]{1,0:T(8,128)(2,1)} %refs_5_.3) | copy-start | bytes 786436
  43.9 37.0 %copy-start.8 = (bf16[256,256]{1,0:T(8,128)(2,1)S(1)}, bf16[256,256]{1,0:T(8,128)(2,1)}, u32[]{:S(2)}) copy-start(bf16[256,256]{1,0:T(8,128)(2,1)} %refs_3_.1) | copy-start | bytes 393220
  43.9 25.3 %collective-permute-start.8 = (bf16[256,512]{1,0:T(8,128)(2,1)S(1)}, bf16[256,512]{1,0:T(8,128)(2,1)S(1)}, u32[]{:S(2)}, u32[]{:S(2)}) collective-permute-start(bf16[256,512]{1,0:T(8,128)(2,1)S(1)} %get-tuple-element.22), channel_id=1, source_target_pairs={{0,4},{4,0},{8,12},{12,8},{16,20},{20,16},{24,28},{28,24},{1,5},{5... | collective-permute-start | bytes 786440 | tf_op jit(solution)/shard_map/ppermute | solution.py:23
  50.0 19.7 %collective-permute-start.17 = (bf16[256,512]{1,0:T(8,128)(2,1)S(1)}, bf16[256,512]{1,0:T(8,128)(2,1)S(1)}, u32[]{:S(2)}, u32[]{:S(2)}) collective-permute-start(bf16[256,512]{1,0:T(8,128)(2,1)S(1)} %get-tuple-element.24), channel_id=1, source_target_pairs={{0,1},{1,0},{2,3},{3,2},{4,5},{5,4},{6,7},{7,6},{8,9},{9,8},{10,11... | collective-permute-start | bytes 786440 | tf_op jit(solution)/shard_map/ppermute | solution.py:23
  53.3 19.3 %collective-permute-start.6 = (bf16[256,512]{1,0:T(8,128)(2,1)S(1)}, bf16[256,512]{1,0:T(8,128)(2,1)S(1)}, u32[]{:S(2)}, u32[]{:S(2)}) collective-permute-start(bf16[256,512]{1,0:T(8,128)(2,1)S(1)} %add_convert_fusion.2), channel_id=1, source_target_pairs={{0,8},{4,12},{8,0},{12,4},{16,24},{20,28},{24,16},{28,20},{1,9},{5... | collective-permute-start | bytes 786440 | tf_op jit(solution)/shard_map/ppermute | solution.py:23
  69.3 12.6 %collective-permute-start.9 = (bf16[256,512]{1,0:T(8,128)(2,1)S(1)}, bf16[256,512]{1,0:T(8,128)(2,1)S(1)}, u32[]{:S(2)}, u32[]{:S(2)}) collective-permute-start(bf16[256,512]{1,0:T(8,128)(2,1)S(1)} %add_convert_fusion), channel_id=1, source_target_pairs={{0,8},{4,12},{8,0},{12,4},{16,24},{20,28},{24,16},{28,20},{1,9},{5... | collective-permute-start | bytes 786440 | tf_op jit(solution)/shard_map/ppermute | solution.py:23
  69.7 6.0 %collective-permute-start.18 = (bf16[256,512]{1,0:T(8,128)(2,1)S(1)}, bf16[256,512]{1,0:T(8,128)(2,1)S(1)}, u32[]{:S(2)}, u32[]{:S(2)}) collective-permute-start(bf16[256,512]{1,0:T(8,128)(2,1)S(1)} %get-tuple-element.26), channel_id=1, source_target_pairs={{0,1},{1,0},{2,3},{3,2},{4,5},{5,4},{6,7},{7,6},{8,9},{9,8},{10,11... | collective-permute-start | bytes 786440 | tf_op jit(solution)/shard_map/ppermute | solution.py:23
  72.1 8.8 %collective-permute-start.19 = (bf16[256,512]{1,0:T(8,128)(2,1)S(1)}, bf16[256,512]{1,0:T(8,128)(2,1)S(1)}, u32[]{:S(2)}, u32[]{:S(2)}) collective-permute-start(bf16[256,512]{1,0:T(8,128)(2,1)S(1)} %get-tuple-element.27), channel_id=1, source_target_pairs={{0,2},{1,3},{2,0},{3,1},{4,6},{5,7},{6,4},{7,5},{8,10},{9,11},{10,... | collective-permute-start | bytes 786440 | tf_op jit(solution)/shard_map/ppermute | solution.py:23
  72.7 15.5 %collective-permute-start.7 = (bf16[256,512]{1,0:T(8,128)(2,1)S(1)}, bf16[256,512]{1,0:T(8,128)(2,1)S(1)}, u32[]{:S(2)}, u32[]{:S(2)}) collective-permute-start(bf16[256,512]{1,0:T(8,128)(2,1)S(1)} %add_convert_fusion.1), channel_id=1, source_target_pairs={{0,16},{4,20},{8,24},{12,28},{16,0},{20,4},{24,8},{28,12},{1,17},{... | collective-permute-start | bytes 786440 | tf_op jit(solution)/shard_map/ppermute | solution.py:23
where the time goes:
time: 89.5 us; the launch traced here: 89.3 us
  waiting for transfers between devices  45.1 us (50%)
  starting transfers between devices  22.7 us (25%)
  Pallas kernels  15.8 us (18%)
  local copies, waits for them, and re-layouts  3.96 us (4%)
  between operations  1.4 us (2%)
    ppermute x20, waiting for transfers between devices, swap(): return lax.ppermute(value, axis, [(i, i ^ mask) for i in range(size)])  45.1 us
    ppermute x20, starting transfers between devices, swap(): return lax.ppermute(value, axis, [(i, i ^ mask) for i in range(size)])  22.7 us
    pallas_call x4, Pallas kernels, multiply(): pl.pallas_call(functools.partial(kernel, parts, len(picks)), in_specs=[in...  9.56 us
    pallas_call x1, Pallas kernels, build(): pl.pallas_call(functools.partial(build_kernel, groups), in_specs=[smem] *...  4.2 us
    unnamed x18, local copies, waits for them, and re-layouts  3.96 us
    pallas_call x2, Pallas kernels, finish(): pl.pallas_call(functools.partial(kernel, len(terms)), in_specs=[in_vmem()...  2.07 us
  transfers between devices with their start and end apart: 20, of which 8 were waited for; matrix products, arithmetic and copies ran while one was open for 0% of the time, Pallas kernels for 17%

commit v1 on v0

--- a/solution.py
+++ b/solution.py
@@ -23,17 +23,8 @@
     return lax.ppermute(value, axis, [(i, i ^ mask) for i in range(size)])
 
 
-def build_kernel(groups, here, rows, cols, count, tiles, dense, held, sems):
-    slots, side, _ = held.shape
-    group = slots // groups
+def clear_kernel(dense):
     height, width = dense.shape
-
-    def fetch(g):
-        part = pl.ds(g * group, group)
-        return pltpu.make_async_copy(tiles.at[part], held.at[part], sems.at[g])
-
-    for g in range(groups):
-        fetch(g).start()
 
     def clear(i, carry):
         dense[pl.ds(pl.multiple_of(i * 32, 32), 32), :] = jnp.zeros((32, width), dense.dtype)
@@ -41,32 +32,44 @@
 
     lax.fori_loop(0, height // 32, clear, 0)
 
-    def place(slot, carry):
-        r, c = rows[slot], cols[slot]
-        r = pl.multiple_of((r ^ here[1]) * side, side)
-        c = pl.multiple_of((c ^ here[0]) * side, side)
-        dense[pl.ds(r, side), pl.ds(c, side)] = held[slot]
-        return carry
-
-    for g in range(groups):
-        fetch(g).wait()
-        lax.fori_loop(g * group, jnp.clip(count[0], g * group, (g + 1) * group), place, 0)
-
-
-def build(here, rows, cols, count, tiles, height, width):
-    slots = tiles.shape[0]
-    groups = max(g for g in range(1, 11) if slots % g == 0)
-    smem = pl.BlockSpec(memory_space=pltpu.SMEM)
-    return pl.pallas_call(
-        functools.partial(build_kernel, groups),
-        in_specs=[smem] * 4 + [pl.BlockSpec(memory_space=pltpu.HBM)],
+
+def clear(height, width):
+    return pl.pallas_call(
+        clear_kernel,
         out_specs=in_vmem(),
         out_shape=jax.ShapeDtypeStruct((height, width), BF16),
-        scratch_shapes=[VMEM(tiles.shape, BF16), pltpu.SemaphoreType.DMA((groups,))],
-        compiler_params=pltpu.CompilerParams(vmem_limit_bytes=8 * 2**20),
+        compiler_params=pltpu.CompilerParams(vmem_limit_bytes=4 * 2**20),
+        cost_estimate=pl.CostEstimate(flops=5 * 10**9, bytes_accessed=height * width * 2, transcendentals=0),
+        name="clear",
+    )()
+
+
+def build_kernel(per_chunk, rows, cols, count, tiles, blank, dense):
+    slots, side, _ = tiles.shape
+    row_flip = lax.axis_index("col") * per_chunk
+    col_flip = lax.axis_index("row") * per_chunk
+
+    def place(slot, carry):
+        r = pl.multiple_of((rows[0, 0, slot] ^ row_flip) * side, side)
+        c = pl.multiple_of((cols[0, 0, slot] ^ col_flip) * side, side)
+        dense[pl.ds(r, side), pl.ds(c, side)] = tiles[slot]
+        return carry
+
+    lax.fori_loop(0, jnp.clip(count[0, 0], 0, slots), place, 0)
+
+
+def build(per_chunk, rows, cols, count, tiles, blank):
+    smem = pl.BlockSpec(memory_space=pltpu.SMEM)
+    return pl.pallas_call(
+        functools.partial(build_kernel, per_chunk),
+        in_specs=[smem] * 3 + [in_vmem()] * 2,
+        out_specs=in_vmem(),
+        out_shape=jax.ShapeDtypeStruct(blank.shape, BF16),
+        input_output_aliases={4: 0},
+        compiler_params=pltpu.CompilerParams(vmem_limit_bytes=4 * 2**20),
         cost_estimate=pl.CostEstimate(flops=5 * 10**9, bytes_accessed=tiles.size * 2, transcendentals=0),
         name="build",
-    )(here, rows, cols, count, tiles)
+    )(rows, cols, count, tiles, blank)
 
 
 def forward_kernel(parts, extra, *refs):
@@ -154,12 +157,9 @@
 
 def per_device(state, adjoint, features, cotangent, mixing, input_weight, tiles, tile_rows, tile_cols, live_tiles):
     n_row, n_col = lax.axis_size("row"), lax.axis_size("col")
-    my_row, my_col = lax.axis_index("row"), lax.axis_index("col")
     hidden, nodes = state.shape
     slab = tiles[0, 0]
     side = slab.shape[-1]
-    per_chunk = nodes // side
-    here = jnp.stack([my_row * per_chunk, my_col * per_chunk]).astype(jnp.int32)
     half_row, half_col = n_row // 2, n_col // 2
     piece = jax.ShapeDtypeStruct((hidden, nodes), BF16)
     wide = jax.ShapeDtypeStruct((hidden, nodes), F32)
@@ -183,19 +183,23 @@
     for block in near:
         states += [block, by_col(block, 1)]
 
-    dense = build(here, tile_rows[0, 0], tile_cols[0, 0], live_tiles[0], slab, n_col * nodes, n_row * nodes)
+    blank = clear(n_col * nodes, n_row * nodes)
+    dense = build(nodes // side, tile_rows, tile_cols, live_tiles, slab, blank)
 
     others = multiply(forward_kernel, states, dense, (), [piece] * half_row)
-    others = [by_row(others[k], 1) for k in range(half_row)]
+    direct = [by_row(others[1], 2)]
+    crossed = {k: by_row(others[k], 1) for k in range(2, half_row)}
     mine = multiply(forward_kernel, states, dense, (input_weight, features), [piece] * half_row + [wide])
     *mine, base = mine
-    flows = [mine[0], others[0]]
+    direct.append(by_row(mine[1], 2))
+    corner = (others[0].astype(F32) + direct[0].astype(F32)).astype(BF16)
+    flows = [mine[0], direct[1], by_row(corner, 1)]
     relayed = None
-    for k in reversed(range(1, half_row)):
-        pair = mine[k].astype(F32) + others[k].astype(F32)
+    for k in reversed(range(2, half_row)):
+        pair = mine[k].astype(F32) + crossed[k].astype(F32)
         if relayed is not None:
             pair = pair + relayed.astype(F32)
-        far = k > 1 and k % 2
+        far = k % 2
         moved = by_row(pair.astype(BF16), 2 if far else 2 * k)
         relayed = moved if far else None
         if not far:

time: 89.5 us -> 71.1 us (0.79)
  waiting for transfers between devices: 45.1 us -> 33.2 us
  local copies, waits for them, and re-layouts: 3.96 us -> 0.05 us
  starting transfers between devices: 22.7 us -> 21 us
  Pallas kernels: 15.8 us -> 14.9 us
    ppermute x20, waiting for transfers between devices: 45.1 us -> 33.2 us  [swap(): return lax.ppermute(value, axis, [(i, i ^ mask) for i in range(size)])]
    unnamed x18 -> x20, local copies, waits for them, and re-layouts: 3.96 us -> 0.05 us
    ppermute x20, starting transfers between devices: 22.7 us -> 21 us  [swap(): return lax.ppermute(value, axis, [(i, i ^ mask) for i in range(size)])]
    pallas_call x1 -> x2, Pallas kernels: 4.2 us -> 3.18 us  [the longest x1 1.97 us: build(): pl.pallas_call(functools.partial(build_kernel, per_chunk), in_specs=[smem...]
  transfers between devices with their start and end apart: 20 -> 20, of which waited for: 8 -> 9; matrix products, arithmetic and copies ran while one was open for 0% -> 0% of each run, Pallas kernels for 17% -> 20%
where the time goes in v1:
time: 71.1 us; the launch traced here: 70.9 us
  waiting for transfers between devices  33.2 us (47%)
  starting transfers between devices  21 us (30%)
  Pallas kernels  14.9 us (21%)
  between operations  1.48 us (2%)
    ppermute x20, waiting for transfers between devices, swap(): return lax.ppermute(value, axis, [(i, i ^ mask) for i in range(size)])  33.2 us
    ppermute x20, starting transfers between devices, swap(): return lax.ppermute(value, axis, [(i, i ^ mask) for i in range(size)])  21 us
    pallas_call x4, Pallas kernels, multiply(): pl.pallas_call(functools.partial(kernel, parts, len(picks)), in_specs=[in...  9.69 us
    pallas_call x2, Pallas kernels, finish(): pl.pallas_call(functools.partial(kernel, len(terms)), in_specs=[in_vmem()...  2.06 us
    pallas_call x1, Pallas kernels, build(): pl.pallas_call(functools.partial(build_kernel, per_chunk), in_specs=[smem...  1.97 us
  transfers between devices with their start and end apart: 20, of which 9 were waited for; matrix products, arithmetic and copies ran while one was open for 0% of the time, Pallas kernels for 20%

profile of v1, /device:TPU:0, one launch (start us, length us, event | category | flops | bytes accessed | tf_op | source)
XLA Modules:
  0.0 70.9 jit_solution(10955856108806451864)
XLA Ops:
  0.7 0.6 collective-permute-start
  1.2 2.6 %collective-permute-start.1 = (bf16[256,512]{1,0:T(8,128)(2,1)}, bf16[256,512]{1,0:T(8,128)(2,1)S(1)}, u32[]{:S(2)}, u32[]{:S(2)}) collective-permute-start(bf16[256,512]{1,0:T(8,128)(2,1)} %refs_4_.3), channel_id=1, source_target_pairs={{0,2},{1,3},{2,0},{3,1},{4,6},{5,7},{6,4},{7,5},{8,10},{9,11},{10,... | collective-permute-start | bytes 786440 | tf_op jit(solution)/shard_map/ppermute | solution.py:23
  3.8 1.5 %collective-permute-start.10 = (bf16[256,512]{1,0:T(8,128)(2,1)}, bf16[256,512]{1,0:T(8,128)(2,1)S(1)}, u32[]{:S(2)}, u32[]{:S(2)}) collective-permute-start(bf16[256,512]{1,0:T(8,128)(2,1)} %refs_0_.7), channel_id=1, source_target_pairs={{0,4},{4,0},{8,12},{12,8},{16,20},{20,16},{24,28},{28,24},{1,5},{5... | collective-permute-start | bytes 786440 | tf_op jit(solution)/shard_map/ppermute | solution.py:23
  5.3 1.6 %collective-permute-start.11 = (bf16[256,512]{1,0:T(8,128)(2,1)}, bf16[256,512]{1,0:T(8,128)(2,1)S(1)}, u32[]{:S(2)}, u32[]{:S(2)}) collective-permute-start(bf16[256,512]{1,0:T(8,128)(2,1)} %refs_0_.7), channel_id=1, source_target_pairs={{0,8},{4,12},{8,0},{12,4},{16,24},{20,28},{24,16},{28,20},{1,9},{5... | collective-permute-start | bytes 786440 | tf_op jit(solution)/shard_map/ppermute | solution.py:23
  6.9 2.6 %collective-permute-start.13 = (bf16[256,512]{1,0:T(8,128)(2,1)}, bf16[256,512]{1,0:T(8,128)(2,1)S(1)}, u32[]{:S(2)}, u32[]{:S(2)}) collective-permute-start(bf16[256,512]{1,0:T(8,128)(2,1)} %refs_0_.7), channel_id=1, source_target_pairs={{0,16},{4,20},{8,24},{12,28},{16,0},{20,4},{24,8},{28,12},{1,17},{... | collective-permute-start | bytes 786440 | tf_op jit(solution)/shard_map/ppermute | solution.py:23
  10.1 1.2 %clear.1.blank = bf16[2048,4096]{1,0:T(8,128)(2,1)S(1)} custom-call(), custom_call_target="tpu_custom_call" | custom-call | flops 5000000000 | bytes 16777216 | tf_op jit(solution)/shard_map/clear/pallas_call | solution.py:37
  11.4 10.0 %collective-permute-done.13.refs_4_ = bf16[256,512]{1,0:T(8,128)(2,1)S(1)} collective-permute-done((bf16[256,512]{1,0:T(8,128)(2,1)}, bf16[256,512]{1,0:T(8,128)(2,1)S(1)}, u32[]{:S(2)}, u32[]{:S(2)}) %collective-permute-start.13) | collective-permute-done | bytes 262176 | tf_op jit(solution)/shard_map/ppermute | solution.py:23
  21.5 0.4 collective-permute-start.15
  21.9 2.0 %build.1.refs_4_.refs_8_ = bf16[2048,4096]{1,0:T(8,128)(2,1)S(1)} custom-call(s32[1,1,170]{2,1,0:T(1,128)S(1)} %copy-done.4, s32[1,1,170]{2,1,0:T(1,128)S(1)} %copy-done.5, s32[1,1]{1,0:T(1,128)S(6)} %copy.14.count, bf16[170,128,128]{2,1,0:T(8,128)(2,1)S(1)} %bitcast.3, bf16[2048,4096]{1,0:T(8,128)(2,1)S(1)} %clear.1.blank), custom_call_target="tpu_custom_call", output_to_operand_aliasing={{}: (4, {})} | custom-call | flops 5000000000 | bytes 5570560 | tf_op jit(solution)/shard_map/build/pallas_call | solution.py:63
  23.9 1.0 %collective-permute-start.14 = (bf16[256,512]{1,0:T(8,128)(2,1)S(1)}, bf16[256,512]{1,0:T(8,128)(2,1)S(1)}, u32[]{:S(2)}, u32[]{:S(2)}) collective-permute-start(bf16[256,512]{1,0:T(8,128)(2,1)S(1)} %collective-permute-done.13.refs_4_), channel_id=1, source_target_pairs={{0,4},{4,0},{8,12},{12,8},{16,20},{20,16},{24,28},{28,24},{1,5},{5... | collective-permute-start | bytes 786440 | tf_op jit(solution)/shard_map/ppermute | solution.py:23
  24.9 1.1 %collective-permute-start.12 = (bf16[256,512]{1,0:T(8,128)(2,1)S(1)}, bf16[256,512]{1,0:T(8,128)(2,1)S(1)}, u32[]{:S(2)}, u32[]{:S(2)}) collective-permute-start(bf16[256,512]{1,0:T(8,128)(2,1)S(1)} %collective-permute-done.11.refs_2_), channel_id=1, source_target_pairs={{0,4},{4,0},{8,12},{12,8},{16,20},{20,16},{24,28},{28,24},{1,5},{5... | collective-permute-start | bytes 786440 | tf_op jit(solution)/shard_map/ppermute | solution.py:23
  26.0 1.8 %collective-permute-done.15.refs_6_ = bf16[256,512]{1,0:T(8,128)(2,1)S(1)} collective-permute-done((bf16[256,512]{1,0:T(8,128)(2,1)S(1)}, bf16[256,512]{1,0:T(8,128)(2,1)S(1)}, u32[]{:S(2)}, u32[]{:S(2)}) %collective-permute-start.15) | collective-permute-done | bytes 262176 | tf_op jit(solution)/shard_map/ppermute | solution.py:23
  27.8 0.5 collective-permute-start.16
  28.4 2.4 %shard_map.114 = (bf16[256,512]{1,0:T(8,128)(2,1)S(1)}, bf16[256,512]{1,0:T(8,128)(2,1)S(1)}, bf16[256,512]{1,0:T(8,128)(2,1)S(1)}, bf16[256,512]{1,0:T(8,128)(2,1)S(1)}) custom-call(bf16[256,512]{1,0:T(8,128)(2,1)S(1)} %copy-done.1, bf16[256,512]{1,0:T(8,128)(2,1)S(1)} %collective-permute-done.refs_1_, bf16[256,512]{1,0:T(8,128)(2,1)S(1)} %collective-permute-done.1.refs_2_, ...), custom_call_target="tpu_custom_call" | custom-call | flops 2147483648 | bytes 8388608 | tf_op jit(solution)/shard_map/pallas_call | solution.py:117
  30.8 1.6 %collective-permute-start.7 = (bf16[256,512]{1,0:T(8,128)(2,1)S(1)}, bf16[256,512]{1,0:T(8,128)(2,1)S(1)}, u32[]{:S(2)}, u32[]{:S(2)}) collective-permute-start(bf16[256,512]{1,0:T(8,128)(2,1)S(1)} %get-tuple-element.22), channel_id=1, source_target_pairs={{0,4},{4,0},{8,12},{12,8},{16,20},{20,16},{24,28},{28,24},{1,5},{5... | collective-permute-start | bytes 786440 | tf_op jit(solution)/shard_map/ppermute | solution.py:23
  32.4 2.5 %shard_map.113 = (bf16[256,512]{1,0:T(8,128)(2,1)S(1)}, bf16[256,512]{1,0:T(8,128)(2,1)S(1)}, bf16[256,512]{1,0:T(8,128)(2,1)S(1)}, bf16[256,512]{1,0:T(8,128)(2,1)S(1)}, f32[256,512]{1,0:T(8,128)S(1)}) custom-call(bf16[256,512]{1,0:T(8,128)(2,1)S(1)} %copy-done.1, bf16[256,512]{1,0:T(8,128)(2,1)S(1)} %collective-permute-done.refs_1_, ...), custom_call_target="tpu_custom_call" | custom-call | flops 2147483648 | bytes 8388608 | tf_op jit(solution)/shard_map/pallas_call | solution.py:117
  34.9 1.3 %collective-permute-start.3 = (bf16[256,512]{1,0:T(8,128)(2,1)S(1)}, bf16[256,512]{1,0:T(8,128)(2,1)S(1)}, u32[]{:S(2)}, u32[]{:S(2)}) collective-permute-start(bf16[256,512]{1,0:T(8,128)(2,1)S(1)} %get-tuple-element.16), channel_id=1, source_target_pairs={{0,8},{4,12},{8,0},{12,4},{16,24},{20,28},{24,16},{28,20},{1,9},{5... | collective-permute-start | bytes 786440 | tf_op jit(solution)/shard_map/ppermute | solution.py:23
  36.2 2.6 %collective-permute-done.12.refs_3_ = bf16[256,512]{1,0:T(8,128)(2,1)S(1)} collective-permute-done((bf16[256,512]{1,0:T(8,128)(2,1)S(1)}, bf16[256,512]{1,0:T(8,128)(2,1)S(1)}, u32[]{:S(2)}, u32[]{:S(2)}) %collective-permute-start.12) | collective-permute-done | bytes 262176 | tf_op jit(solution)/shard_map/ppermute | solution.py:23
  38.8 1.4 %collective-permute-start.4 = (bf16[256,512]{1,0:T(8,128)(2,1)S(1)}, bf16[256,512]{1,0:T(8,128)(2,1)S(1)}, u32[]{:S(2)}, u32[]{:S(2)}) collective-permute-start(bf16[256,512]{1,0:T(8,128)(2,1)S(1)} %get-tuple-element.18), channel_id=1, source_target_pairs={{0,8},{4,12},{8,0},{12,4},{16,24},{20,28},{24,16},{28,20},{1,9},{5... | collective-permute-start | bytes 786440 | tf_op jit(solution)/shard_map/ppermute | solution.py:23
  40.2 0.9 %collective-permute-start.6 = (bf16[256,512]{1,0:T(8,128)(2,1)S(1)}, bf16[256,512]{1,0:T(8,128)(2,1)S(1)}, u32[]{:S(2)}, u32[]{:S(2)}) collective-permute-start(bf16[256,512]{1,0:T(8,128)(2,1)S(1)} %get-tuple-element.20), channel_id=1, source_target_pairs={{0,4},{4,0},{8,12},{12,8},{16,20},{20,16},{24,28},{28,24},{1,5},{5... | collective-permute-start | bytes 786440 | tf_op jit(solution)/shard_map/ppermute | solution.py:23
  41.1 3.3 %collective-permute-done.16.refs_7_ = bf16[256,512]{1,0:T(8,128)(2,1)S(1)} collective-permute-done((bf16[256,512]{1,0:T(8,128)(2,1)S(1)}, bf16[256,512]{1,0:T(8,128)(2,1)S(1)}, u32[]{:S(2)}, u32[]{:S(2)}) %collective-permute-start.16) | collective-permute-done | bytes 262176 | tf_op jit(solution)/shard_map/ppermute | solution.py:23
  44.4 2.4 %shard_map.116 = (bf16[256,512]{1,0:T(8,128)(2,1)S(1)}, bf16[256,512]{1,0:T(8,128)(2,1)S(1)}) custom-call(bf16[256,512]{1,0:T(8,128)(2,1)S(1)} %copy-done, bf16[256,512]{1,0:T(8,128)(2,1)S(1)} %collective-permute-done.10.refs_1_, bf16[256,512]{1,0:T(8,128)(2,1)S(1)} %collective-permute-done.11.refs_2_, bf16[256,512]{1,0:T(8,128)(2,1)S(1)} %collective-permute-done.12.refs_3_, ...), custom_call_target="tpu_custom_call" | custom-call | flops 2147483648 | bytes 8388608 | tf_op jit(solution)/shard_map/pallas_call | solution.py:117
  46.9 3.2 %collective-permute-done.7 = bf16[256,512]{1,0:T(8,128)(2,1)S(1)} collective-permute-done((bf16[256,512]{1,0:T(8,128)(2,1)S(1)}, bf16[256,512]{1,0:T(8,128)(2,1)S(1)}, u32[]{:S(2)}, u32[]{:S(2)}) %collective-permute-start.7) | collective-permute-done | bytes 262176 | tf_op jit(solution)/shard_map/ppermute | solution.py:23
  50.1 1.3 %collective-permute-start.8 = (bf16[256,512]{1,0:T(8,128)(2,1)S(1)}, bf16[256,512]{1,0:T(8,128)(2,1)S(1)}, u32[]{:S(2)}, u32[]{:S(2)}) collective-permute-start(bf16[256,512]{1,0:T(8,128)(2,1)S(1)} %add_convert_fusion.1), channel_id=1, source_target_pairs={{0,8},{4,12},{8,0},{12,4},{16,24},{20,28},{24,16},{28,20},{1,9},{5... | collective-permute-start | bytes 786440 | tf_op jit(solution)/shard_map/ppermute | solution.py:23
  51.8 2.4 %shard_map.117 = (bf16[256,512]{1,0:T(8,128)(2,1)S(1)}, bf16[256,512]{1,0:T(8,128)(2,1)S(1)}) custom-call(bf16[256,512]{1,0:T(8,128)(2,1)S(1)} %copy-done, bf16[256,512]{1,0:T(8,128)(2,1)S(1)} %collective-permute-done.10.refs_1_, bf16[256,512]{1,0:T(8,128)(2,1)S(1)} %collective-permute-done.11.refs_2_, bf16[256,512]{1,0:T(8,128)(2,1)S(1)} %collective-permute-done.12.refs_3_, ...), custom_call_target="tpu_custom_call" | custom-call | flops 2147483648 | bytes 8388608 | tf_op jit(solution)/shard_map/pallas_call | solution.py:117
  54.2 1.5 %collective-permute-done.6 = bf16[256,512]{1,0:T(8,128)(2,1)S(1)} collective-permute-done((bf16[256,512]{1,0:T(8,128)(2,1)S(1)}, bf16[256,512]{1,0:T(8,128)(2,1)S(1)}, u32[]{:S(2)}, u32[]{:S(2)}) %collective-permute-start.6) | collective-permute-done | bytes 262176 | tf_op jit(solution)/shard_map/ppermute | solution.py:23
  55.7 0.9 %collective-permute-done.8 = bf16[256,512]{1,0:T(8,128)(2,1)S(1)} collective-permute-done((bf16[256,512]{1,0:T(8,128)(2,1)S(1)}, bf16[256,512]{1,0:T(8,128)(2,1)S(1)}, u32[]{:S(2)}, u32[]{:S(2)}) %collective-permute-start.8) | collective-permute-done | bytes 262176 | tf_op jit(solution)/shard_map/ppermute | solution.py:23
  56.7 2.3 %collective-permute-start.9 = (bf16[256,512]{1,0:T(8,128)(2,1)S(1)}, bf16[256,512]{1,0:T(8,128)(2,1)S(1)}, u32[]{:S(2)}, u32[]{:S(2)}) collective-permute-start(bf16[256,512]{1,0:T(8,128)(2,1)S(1)} %add_convert_fusion), channel_id=1, source_target_pairs={{0,16},{4,20},{8,24},{12,28},{16,0},{20,4},{24,8},{28,12},{1,17},{... | collective-permute-start | bytes 786440 | tf_op jit(solution)/shard_map/ppermute | solution.py:23
  59.0 4.0 %collective-permute-done.19.refs_2_ = bf16[256,512]{1,0:T(8,128)(2,1)S(1)} collective-permute-done((bf16[256,512]{1,0:T(8,128)(2,1)S(1)}, bf16[256,512]{1,0:T(8,128)(2,1)S(1)}, u32[]{:S(2)}, u32[]{:S(2)}) %collective-permute-start.19) | collective-permute-done | bytes 262176 | tf_op jit(solution)/shard_map/ppermute | solution.py:23
  63.0 1.0 %shard_map.118 = bf16[256,512]{1,0:T(8,128)(2,1)} custom-call(bf16[256,512]{1,0:T(8,128)(2,1)S(1)} %get-tuple-element.25.refs_0_, bf16[256,512]{1,0:T(8,128)(2,1)S(1)} %collective-permute-done.18.refs_1_, bf16[256,512]{1,0:T(8,128)(2,1)S(1)} %collective-permute-done.19.refs_2_, bf16[256,256]{1,0:T(8,128)(2,1)S(1)} %copy-done.7, ...), custom_call_target="tpu_custom_call" | custom-call | flops 1000000000 | bytes 2097152 | tf_op jit(solution)/shard_map/pallas_call | solution.py:148
  64.0 5.8 %collective-permute-done.9.refs_3_ = bf16[256,512]{1,0:T(8,128)(2,1)S(1)} collective-permute-done((bf16[256,512]{1,0:T(8,128)(2,1)S(1)}, bf16[256,512]{1,0:T(8,128)(2,1)S(1)}, u32[]{:S(2)}, u32[]{:S(2)}) %collective-permute-start.9) | collective-permute-done | bytes 262176 | tf_op jit(solution)/shard_map/ppermute | solution.py:23
  69.9 1.0 %shard_map.115 = bf16[256,512]{1,0:T(8,128)(2,1)} custom-call(bf16[256,512]{1,0:T(8,128)(2,1)S(1)} %get-tuple-element.15.refs_0_, bf16[256,512]{1,0:T(8,128)(2,1)S(1)} %collective-permute-done.3.refs_1_, bf16[256,512]{1,0:T(8,128)(2,1)S(1)} %collective-permute-done.5.refs_2_, bf16[256,512]{1,0:T(8,128)(2,1)S(1)} %collective-permute-done.9.refs_3_, ...), custom_call_target="tpu_custom_call" | custom-call | flops 1000000000 | bytes 2097152 | tf_op jit(solution)/shard_map/pallas_call | solution.py:148
  (40 shorter events, 0.8 us)
Async XLA Ops:
  0.6 21.3 %copy-start.4 = (s32[1,1,170]{2,1,0:T(1,128)S(1)}, s32[1,1,170]{2,1,0:T(1,128)}, u32[]{:S(2)}) copy-start(s32[1,1,170]{2,1,0:T(1,128)} %rows.1) | copy-start | bytes 2044
  0.6 21.3 %copy-start.5 = (s32[1,1,170]{2,1,0:T(1,128)S(1)}, s32[1,1,170]{2,1,0:T(1,128)}, u32[]{:S(2)}) copy-start(s32[1,1,170]{2,1,0:T(1,128)} %cols.1) | copy-start | bytes 2044
  0.7 21.3 %slice-start = ((s8[5570560]{0:T(1024)(128)(4,1)}), s8[4194304]{0:T(1024)(128)(4,1)S(1)}, s32[]{:S(2)}) async-start(s8[5570560]{0:T(1024)(128)(4,1)} %bitcast.1), calls=%async_computation | async-start | bytes 8388608
  0.7 23.3 %collective-permute-start = (bf16[256,512]{1,0:T(8,128)(2,1)}, bf16[256,512]{1,0:T(8,128)(2,1)S(1)}, u32[]{:S(2)}, u32[]{:S(2)}) collective-permute-start(bf16[256,512]{1,0:T(8,128)(2,1)} %refs_4_.3), channel_id=1, source_target_pairs={{0,1},{1,0},{2,3},{3,2},{4,5},{5,4},{6,7},{7,6},{8,9},{9,8},{10,11... | collective-permute-start | bytes 786440 | tf_op jit(solution)/shard_map/ppermute | solution.py:23
  1.2 10.1 %collective-permute-start.1 = (bf16[256,512]{1,0:T(8,128)(2,1)}, bf16[256,512]{1,0:T(8,128)(2,1)S(1)}, u32[]{:S(2)}, u32[]{:S(2)}) collective-permute-start(bf16[256,512]{1,0:T(8,128)(2,1)} %refs_4_.3), channel_id=1, source_target_pairs={{0,2},{1,3},{2,0},{3,1},{4,6},{5,7},{6,4},{7,5},{8,10},{9,11},{10,... | collective-permute-start | bytes 786440 | tf_op jit(solution)/shard_map/ppermute | solution.py:23
  3.8 31.1 %collective-permute-start.10 = (bf16[256,512]{1,0:T(8,128)(2,1)}, bf16[256,512]{1,0:T(8,128)(2,1)S(1)}, u32[]{:S(2)}, u32[]{:S(2)}) collective-permute-start(bf16[256,512]{1,0:T(8,128)(2,1)} %refs_0_.7), channel_id=1, source_target_pairs={{0,4},{4,0},{8,12},{12,8},{16,20},{20,16},{24,28},{28,24},{1,5},{5... | collective-permute-start | bytes 786440 | tf_op jit(solution)/shard_map/ppermute | solution.py:23
  5.3 19.6 %collective-permute-start.11 = (bf16[256,512]{1,0:T(8,128)(2,1)}, bf16[256,512]{1,0:T(8,128)(2,1)S(1)}, u32[]{:S(2)}, u32[]{:S(2)}) collective-permute-start(bf16[256,512]{1,0:T(8,128)(2,1)} %refs_0_.7), channel_id=1, source_target_pairs={{0,8},{4,12},{8,0},{12,4},{16,24},{20,28},{24,16},{28,20},{1,9},{5... | collective-permute-start | bytes 786440 | tf_op jit(solution)/shard_map/ppermute | solution.py:23
  6.9 14.6 %collective-permute-start.13 = (bf16[256,512]{1,0:T(8,128)(2,1)}, bf16[256,512]{1,0:T(8,128)(2,1)S(1)}, u32[]{:S(2)}, u32[]{:S(2)}) collective-permute-start(bf16[256,512]{1,0:T(8,128)(2,1)} %refs_0_.7), channel_id=1, source_target_pairs={{0,16},{4,20},{8,24},{12,28},{16,0},{20,4},{24,8},{28,12},{1,17},{... | collective-permute-start | bytes 786440 | tf_op jit(solution)/shard_map/ppermute | solution.py:23
  10.1 11.8 %slice-start.1 = ((s8[5570560]{0:T(1024)(128)(4,1)}), s8[1376256]{0:T(1024)(128)(4,1)S(1)}, s32[]{:S(2)}) async-start(s8[5570560]{0:T(1024)(128)(4,1)} %bitcast.1), calls=%async_computation.1 | async-start | bytes 2752512
  11.4 17.0 %collective-permute-start.2 = (bf16[256,512]{1,0:T(8,128)(2,1)S(1)}, bf16[256,512]{1,0:T(8,128)(2,1)S(1)}, u32[]{:S(2)}, u32[]{:S(2)}) collective-permute-start(bf16[256,512]{1,0:T(8,128)(2,1)S(1)} %collective-permute-done.1.refs_2_), channel_id=1, source_target_pairs={{0,1},{1,0},{2,3},{3,2},{4,5},{5,4},{6,7},{7,6},{8,9},{9,8},{10,11... | collective-permute-start | bytes 786440 | tf_op jit(solution)/shard_map/ppermute | solution.py:23
  21.5 6.4 %collective-permute-start.15 = (bf16[256,512]{1,0:T(8,128)(2,1)S(1)}, bf16[256,512]{1,0:T(8,128)(2,1)S(1)}, u32[]{:S(2)}, u32[]{:S(2)}) collective-permute-start(bf16[256,512]{1,0:T(8,128)(2,1)S(1)} %collective-permute-done.13.refs_4_), channel_id=1, source_target_pairs={{0,8},{4,12},{8,0},{12,4},{16,24},{20,28},{24,16},{28,20},{1,9},{5... | collective-permute-start | bytes 786440 | tf_op jit(solution)/shard_map/ppermute | solution.py:23
  21.9 6.5 %copy-start.1 = (bf16[256,512]{1,0:T(8,128)(2,1)S(1)}, bf16[256,512]{1,0:T(8,128)(2,1)}, u32[]{:S(2)}) copy-start(bf16[256,512]{1,0:T(8,128)(2,1)} %refs_4_.3) | copy-start | bytes 786436
  23.9 8.5 %copy-start.2 = (bf16[128,512]{1,0:T(8,128)(2,1)S(1)}, bf16[128,512]{1,0:T(8,128)(2,1)}, u32[]{:S(2)}) copy-start(bf16[128,512]{1,0:T(8,128)(2,1)} %refs_6_.1) | copy-start | bytes 393220
  23.9 8.5 %copy-start.3 = (bf16[256,128]{1,0:T(8,128)(2,1)S(1)}, bf16[256,128]{1,0:T(8,128)(2,1)}, u32[]{:S(2)}) copy-start(bf16[256,128]{1,0:T(8,128)(2,1)} %refs_5_.2) | copy-start | bytes 196612
  23.9 20.5 %copy-start = (bf16[256,512]{1,0:T(8,128)(2,1)S(1)}, bf16[256,512]{1,0:T(8,128)(2,1)}, u32[]{:S(2)}) copy-start(bf16[256,512]{1,0:T(8,128)(2,1)} %refs_0_.7) | copy-start | bytes 786436
  23.9 16.2 %collective-permute-start.14 = (bf16[256,512]{1,0:T(8,128)(2,1)S(1)}, bf16[256,512]{1,0:T(8,128)(2,1)S(1)}, u32[]{:S(2)}, u32[]{:S(2)}) collective-permute-start(bf16[256,512]{1,0:T(8,128)(2,1)S(1)} %collective-permute-done.13.refs_4_), channel_id=1, source_target_pairs={{0,4},{4,0},{8,12},{12,8},{16,20},{20,16},{24,28},{28,24},{1,5},{5... | collective-permute-start | bytes 786440 | tf_op jit(solution)/shard_map/ppermute | solution.py:23
  24.9 13.9 %collective-permute-start.12 = (bf16[256,512]{1,0:T(8,128)(2,1)S(1)}, bf16[256,512]{1,0:T(8,128)(2,1)S(1)}, u32[]{:S(2)}, u32[]{:S(2)}) collective-permute-start(bf16[256,512]{1,0:T(8,128)(2,1)S(1)} %collective-permute-done.11.refs_2_), channel_id=1, source_target_pairs={{0,4},{4,0},{8,12},{12,8},{16,20},{20,16},{24,28},{28,24},{1,5},{5... | collective-permute-start | bytes 786440 | tf_op jit(solution)/shard_map/ppermute | solution.py:23
  27.8 16.6 %collective-permute-start.16 = (bf16[256,512]{1,0:T(8,128)(2,1)S(1)}, bf16[256,512]{1,0:T(8,128)(2,1)S(1)}, u32[]{:S(2)}, u32[]{:S(2)}) collective-permute-start(bf16[256,512]{1,0:T(8,128)(2,1)S(1)} %collective-permute-done.15.refs_6_), channel_id=1, source_target_pairs={{0,4},{4,0},{8,12},{12,8},{16,20},{20,16},{24,28},{28,24},{1,5},{5... | collective-permute-start | bytes 786440 | tf_op jit(solution)/shard_map/ppermute | solution.py:23
  30.8 19.2 %collective-permute-start.7 = (bf16[256,512]{1,0:T(8,128)(2,1)S(1)}, bf16[256,512]{1,0:T(8,128)(2,1)S(1)}, u32[]{:S(2)}, u32[]{:S(2)}) collective-permute-start(bf16[256,512]{1,0:T(8,128)(2,1)S(1)} %get-tuple-element.22), channel_id=1, source_target_pairs={{0,4},{4,0},{8,12},{12,8},{16,20},{20,16},{24,28},{28,24},{1,5},{5... | collective-permute-start | bytes 786440 | tf_op jit(solution)/shard_map/ppermute | solution.py:23
  34.9 29.1 %collective-permute-start.3 = (bf16[256,512]{1,0:T(8,128)(2,1)S(1)}, bf16[256,512]{1,0:T(8,128)(2,1)S(1)}, u32[]{:S(2)}, u32[]{:S(2)}) collective-permute-start(bf16[256,512]{1,0:T(8,128)(2,1)S(1)} %get-tuple-element.16), channel_id=1, source_target_pairs={{0,8},{4,12},{8,0},{12,4},{16,24},{20,28},{24,16},{28,20},{1,9},{5... | collective-permute-start | bytes 786440 | tf_op jit(solution)/shard_map/ppermute | solution.py:23
  38.8 12.6 %collective-permute-start.4 = (bf16[256,512]{1,0:T(8,128)(2,1)S(1)}, bf16[256,512]{1,0:T(8,128)(2,1)S(1)}, u32[]{:S(2)}, u32[]{:S(2)}) collective-permute-start(bf16[256,512]{1,0:T(8,128)(2,1)S(1)} %get-tuple-element.18), channel_id=1, source_target_pairs={{0,8},{4,12},{8,0},{12,4},{16,24},{20,28},{24,16},{28,20},{1,9},{5... | collective-permute-start | bytes 786440 | tf_op jit(solution)/shard_map/ppermute | solution.py:23
  40.2 22.8 %copy-start.6 = (bf16[256,512]{1,0:T(8,128)(2,1)S(1)}, bf16[256,512]{1,0:T(8,128)(2,1)}, u32[]{:S(2)}) copy-start(bf16[256,512]{1,0:T(8,128)(2,1)} %refs_5_.3) | copy-start | bytes 786436
  40.2 22.8 %copy-start.7 = (bf16[256,256]{1,0:T(8,128)(2,1)S(1)}, bf16[256,256]{1,0:T(8,128)(2,1)}, u32[]{:S(2)}) copy-start(bf16[256,256]{1,0:T(8,128)(2,1)} %refs_3_.1) | copy-start | bytes 393220
  40.2 15.5 %collective-permute-start.6 = (bf16[256,512]{1,0:T(8,128)(2,1)S(1)}, bf16[256,512]{1,0:T(8,128)(2,1)S(1)}, u32[]{:S(2)}, u32[]{:S(2)}) collective-permute-start(bf16[256,512]{1,0:T(8,128)(2,1)S(1)} %get-tuple-element.20), channel_id=1, source_target_pairs={{0,4},{4,0},{8,12},{12,8},{16,20},{20,16},{24,28},{28,24},{1,5},{5... | collective-permute-start | bytes 786440 | tf_op jit(solution)/shard_map/ppermute | solution.py:23
  46.8 5.0 %collective-permute-start.17 = (bf16[256,512]{1,0:T(8,128)(2,1)S(1)}, bf16[256,512]{1,0:T(8,128)(2,1)S(1)}, u32[]{:S(2)}, u32[]{:S(2)}) collective-permute-start(bf16[256,512]{1,0:T(8,128)(2,1)S(1)} %get-tuple-element.24), channel_id=1, source_target_pairs={{0,1},{1,0},{2,3},{3,2},{4,5},{5,4},{6,7},{7,6},{8,9},{9,8},{10,11... | collective-permute-start | bytes 786440 | tf_op jit(solution)/shard_map/ppermute | solution.py:23
  50.1 6.4 %collective-permute-start.8 = (bf16[256,512]{1,0:T(8,128)(2,1)S(1)}, bf16[256,512]{1,0:T(8,128)(2,1)S(1)}, u32[]{:S(2)}, u32[]{:S(2)}) collective-permute-start(bf16[256,512]{1,0:T(8,128)(2,1)S(1)} %add_convert_fusion.1), channel_id=1, source_target_pairs={{0,8},{4,12},{8,0},{12,4},{16,24},{20,28},{24,16},{28,20},{1,9},{5... | collective-permute-start | bytes 786440 | tf_op jit(solution)/shard_map/ppermute | solution.py:23
  51.5 12.6 %collective-permute-start.5 = (bf16[256,512]{1,0:T(8,128)(2,1)S(1)}, bf16[256,512]{1,0:T(8,128)(2,1)S(1)}, u32[]{:S(2)}, u32[]{:S(2)}) collective-permute-start(bf16[256,512]{1,0:T(8,128)(2,1)S(1)} %add_convert_fusion.2), channel_id=1, source_target_pairs={{0,4},{4,0},{8,12},{12,8},{16,20},{20,16},{24,28},{28,24},{1,5},{5... | collective-permute-start | bytes 786440 | tf_op jit(solution)/shard_map/ppermute | solution.py:23
  51.8 7.1 %collective-permute-start.18 = (bf16[256,512]{1,0:T(8,128)(2,1)S(1)}, bf16[256,512]{1,0:T(8,128)(2,1)S(1)}, u32[]{:S(2)}, u32[]{:S(2)}) collective-permute-start(bf16[256,512]{1,0:T(8,128)(2,1)S(1)} %get-tuple-element.26), channel_id=1, source_target_pairs={{0,1},{1,0},{2,3},{3,2},{4,5},{5,4},{6,7},{7,6},{8,9},{9,8},{10,11... | collective-permute-start | bytes 786440 | tf_op jit(solution)/shard_map/ppermute | solution.py:23
  55.7 7.3 %collective-permute-start.19 = (bf16[256,512]{1,0:T(8,128)(2,1)S(1)}, bf16[256,512]{1,0:T(8,128)(2,1)S(1)}, u32[]{:S(2)}, u32[]{:S(2)}) collective-permute-start(bf16[256,512]{1,0:T(8,128)(2,1)S(1)} %get-tuple-element.27), channel_id=1, source_target_pairs={{0,2},{1,3},{2,0},{3,1},{4,6},{5,7},{6,4},{7,5},{8,10},{9,11},{10,... | collective-permute-start | bytes 786440 | tf_op jit(solution)/shard_map/ppermute | solution.py:23
  56.7 13.2 %collective-permute-start.9 = (bf16[256,512]{1,0:T(8,128)(2,1)S(1)}, bf16[256,512]{1,0:T(8,128)(2,1)S(1)}, u32[]{:S(2)}, u32[]{:S(2)}) collective-permute-start(bf16[256,512]{1,0:T(8,128)(2,1)S(1)} %add_convert_fusion), channel_id=1, source_target_pairs={{0,16},{4,20},{8,24},{12,28},{16,0},{20,4},{24,8},{28,12},{1,17},{... | collective-permute-start | bytes 786440 | tf_op jit(solution)/shard_map/ppermute | solution.py:23
